TPU v7x, 512 devices: a whole 4x8x8 slice. The times are simulated.
512 devices in a mesh: req: 64 (over y, x, z_lo), tp: 8 (over z_hi, core).
Axes of the slice: x: 4, y: 8, z: 8 (z_hi: 4, z_lo: 2; z = z_hi * 2 + z_lo), core: 2. Of those that a mesh axis runs over, the one named last changes fastest.
Arguments:
- tree_queries: bfloat16 [64, 512, 4096], P('req', None, 'tp'), may hold values from -512 to 512
- tree_keys: bfloat16 [64, 512, 512], P('req', None, 'tp'), may hold values from -6 to 6
- tree_values: bfloat16 [64, 512, 512], P('req', None, 'tp'), may hold values from -6 to 6
- cache_keys: bfloat16 [64, 1024, 512], P('req', None, 'tp'), may hold values from -6 to 6
- cache_values: bfloat16 [64, 1024, 512], P('req', None, 'tp'), may hold values from -6 to 6
- sinks: float32 [64], P('tp'), may hold values from 7 to 11
- parents: int32 [64, 512], P('req'), may hold values from 0 to 510, as said below
- tile_counts: int32 [64], P('req'), may hold values from 1 to 4, 128 in all
- out_weight: bfloat16 [4096, 2880], P('tp', 'req'), may hold values from -0.71875 to 0.71875
Outputs:
- mixed: bfloat16 [64, 512, 2880], P('req', 'tp')
Inputs may be any that keep to these rules, and one draw needn't show every extreme that they name: `parents`: each position's parent stands before it; position 0 is its own parent. `tile_counts`: the counts sum to 128.
All inputs are finite; a program needn't handle non-finite values. No bound on the sum of `tile_counts` on one device may be relied on, other than what follows from the above.
Results may differ from a plain program's by a relative error of at most 0.024.
Values may be sent and summed in bfloat16 or wider, within the bound.
A program may use at most 64 MiB of HBM per device.

v0:
```python
import jax
import jax.numpy as jnp
from jax import lax
from jax.sharding import Mesh
from jax.sharding import PartitionSpec as P

HEADS = 64
KV_HEADS = 8
HEAD_DIM = 64
TREE = 512
TILE = 128
REQ = ("req_0", "req_1", "req_2")


masked_score = -1e30


def piece_ends(length, count):
    hop = length // count
    if hop >= 8:
        hop -= hop % 8
    return [hop * k for k in range(1, count)]


def all_blocks(x, axes, order):
    parts = x[None]
    for k in order:
        parts = lax.all_gather(parts, axes[k], axis=0, tiled=True)
    block = [lax.axis_size(axes[k]) for k in reversed(order)]
    parts = parts.reshape(*block, *x.shape)
    turned = sorted(range(len(order)), key=lambda place: order[len(order) - 1 - place])
    return parts.transpose(*turned, *range(len(order), parts.ndim)).reshape(-1, *x.shape)


def in_order(parts, dim):
    parts = jnp.moveaxis(parts, 0, dim)
    dims = parts.shape
    return parts.reshape(*dims[:dim], dims[dim] * dims[dim + 1], *dims[dim + 2 :])


def spread_gather(x, axes, dim):
    numbers = list(range(len(axes)))[::-1]
    split_at = x.shape.index(max(x.shape[:-1] or x.shape))
    edges = [0, *piece_ends(x.shape[split_at], len(axes)), x.shape[split_at]]
    done = []
    for k, (start, end) in enumerate(zip(edges, edges[1:])):
        if end > start:
            share = lax.slice_in_dim(x, start, end, axis=split_at)
            done.append(all_blocks(share, axes, numbers[k:] + numbers[:k]))
    return in_order(jnp.concatenate(done, axis=split_at + 1), dim)


def ancestry(parents):
    length = parents.shape[0]
    upward = parents
    visible = jnp.eye(length, dtype=jnp.int32)
    doubling = 0
    while 1 << doubling < length:
        visible = jnp.maximum(visible, jnp.take(visible, upward, axis=0))
        upward = jnp.take(upward, upward, axis=0)
        doubling += 1
    return visible


def block_stats(tile_rows, key_rows, value_rows, allowed):
    scaling = tile_rows.shape[-1] ** (-0.5)
    scores = (
        jnp.einsum("tkgd,ckd->kgtc", tile_rows, key_rows, preferred_element_type=jnp.float32)
        * scaling
    )
    if allowed is not None:
        scores = jnp.where(allowed[None, None], scores, masked_score)
    maxima = scores.max(-1)
    weights = jnp.exp(scores - maxima[..., None])
    totals = weights.sum(-1)
    weighted = jnp.einsum(
        "kgtc,ckd->kgtd",
        weights.astype(jnp.bfloat16),
        value_rows,
        preferred_element_type=jnp.float32,
    )
    return (maxima, totals, weighted)


def combine(first, second):
    maxima = jnp.maximum(first[0], second[0])
    left_scale = jnp.exp(first[0] - maxima)
    right_scale = jnp.exp(second[0] - maxima)
    totals = first[1] * left_scale + second[1] * right_scale
    weighted = first[2] * left_scale[..., None] + second[2] * right_scale[..., None]
    return (maxima, totals, weighted)


def empty_stats(tile_rows):
    grid_shape = (tile_rows.shape[1], tile_rows.shape[2], tile_rows.shape[0])
    return (
        jnp.full(grid_shape, masked_score, jnp.float32),
        jnp.zeros(grid_shape, jnp.float32),
        jnp.zeros(grid_shape + (tile_rows.shape[3],), jnp.float32),
    )


def cache_stats(tile_rows, key_rows, value_rows):
    length = key_rows.shape[0]
    block_size = min(512, length)
    blocks = length // block_size
    key_blocks = key_rows.reshape(blocks, block_size, key_rows.shape[1], key_rows.shape[2])
    value_blocks = value_rows.reshape(blocks, block_size, value_rows.shape[1], value_rows.shape[2])

    def advance(running, block_pair):
        return (combine(running, block_stats(tile_rows, block_pair[0], block_pair[1], None)), None)

    running, unused = lax.scan(advance, empty_stats(tile_rows), (key_blocks, value_blocks))
    return running


def finish(stats, sink_grid):
    maxima = jnp.maximum(stats[0], sink_grid[:, :, None])
    rescale = jnp.exp(stats[0] - maxima)
    denominator = stats[1] * rescale + jnp.exp(sink_grid[:, :, None] - maxima)
    attention = stats[2] * (rescale / denominator)[..., None]
    tile_length = attention.shape[2]
    return attention.transpose(2, 0, 1, 3).reshape(tile_length, -1).astype(jnp.bfloat16)


def per_device(
    tree_queries,
    tree_keys,
    tree_values,
    cache_keys,
    cache_values,
    sinks,
    parents,
    tile_counts,
    out_weight,
):
    queries = tree_queries[0]
    kv_local = cache_keys.shape[2] // HEAD_DIM
    group_size = HEADS // KV_HEADS
    tree_k = tree_keys[0].reshape(TREE, kv_local, HEAD_DIM)
    tree_v = tree_values[0].reshape(TREE, kv_local, HEAD_DIM)
    cache_k = cache_keys[0].reshape(-1, kv_local, HEAD_DIM)
    cache_v = cache_values[0].reshape(-1, kv_local, HEAD_DIM)
    sink_grid = sinks.reshape(kv_local, group_size)
    visible = ancestry(parents[0])
    live_tiles = tile_counts[0]
    tile_total = TREE // TILE
    zeros_out = jnp.zeros((TILE, kv_local * group_size * HEAD_DIM), jnp.bfloat16)

    def tile_queries(source, tile_index):
        return source[tile_index * TILE : (tile_index + 1) * TILE].reshape(
            TILE, kv_local, group_size, HEAD_DIM
        )

    def own_stats(tile_index, key_rows, value_rows):
        tile_rows = tile_queries(queries, tile_index)
        allowed = visible[tile_index * TILE : (tile_index + 1) * TILE] > 0
        return combine(
            cache_stats(tile_rows, key_rows, value_rows),
            block_stats(tile_rows, tree_k, tree_v, allowed),
        )

    outputs = []
    for tile_index in range(tile_total):
        outputs.append(
            lax.cond(
                tile_index < live_tiles,
                lambda: finish(own_stats(tile_index, cache_k, cache_v), sink_grid),
                lambda: zeros_out,
            )
        )
    attention = jnp.concatenate(outputs, 0)
    terms = jnp.dot(
        attention, spread_gather(out_weight, REQ, 1), preferred_element_type=jnp.float32
    )
    mixed = lax.psum_scatter(terms.astype(jnp.bfloat16), "tp", scatter_dimension=0, tiled=True)
    return mixed[None]


def solution(mesh):
    split = Mesh(mesh.devices.reshape(8, 4, 2, mesh.shape["tp"]), ("req_0", "req_1", "req_2", "tp"))
    placed = (
        P(REQ, None, "tp"),
        P(REQ, None, "tp"),
        P(REQ, None, "tp"),
        P(REQ, None, "tp"),
        P(REQ, None, "tp"),
        P("tp"),
        P(REQ, None),
        P(REQ),
        P("tp", REQ),
    )
    return jax.shard_map(
        per_device, mesh=split, in_specs=placed, out_specs=P(REQ, "tp", None), check_vma=False
    )
```

profile of v0, /device:TPU:1, one launch (start us, length us, event | category | flops | bytes accessed | tf_op | source)
XLA Modules:
  0.0 317.4 jit_solution(7874271407768890003)
XLA Ops:
  6.5 0.8 slice_bitcast_fusion
  7.4 0.9 slice_bitcast_fusion.2
  9.1 0.7 compare_select_fusion.8
  9.8 3.5 %gather_fusion.1 = s32[512]{0:T(512)S(1)} fusion(s32[512]{0:T(512)S(1)} %bitcast.602, s32[1024]{0:T(1024)S(1)} %pad_clamp_fusion.8), kind=kCustom, calls=%fused_computation.1.clone | custom fusion | bytes 6144 | tf_op jit(solution)/shard_map/jit(_take)/gather | solution.py:60
  13.3 3.5 %gather_fusion.3 = s32[512]{0:T(512)S(1)} fusion(s32[512]{0:T(512)S(1)} %get-tuple-element.637, s32[1024]{0:T(1024)S(1)} %pad_clamp_fusion.7), kind=kCustom, calls=%fused_computation.10.clone | custom fusion | bytes 6144 | tf_op jit(solution)/shard_map/jit(_take)/gather | solution.py:60
  16.8 3.5 %gather_fusion.5 = s32[512]{0:T(512)S(1)} fusion(s32[512]{0:T(512)S(1)} %get-tuple-element.634, s32[1024]{0:T(1024)S(1)} %pad_clamp_fusion.6), kind=kCustom, calls=%fused_computation.11.clone | custom fusion | bytes 6144 | tf_op jit(solution)/shard_map/jit(_take)/gather | solution.py:60
  20.3 0.5 compare_select_fusion.5
  20.9 3.5 %gather_fusion.7 = s32[512]{0:T(512)S(1)} fusion(s32[512]{0:T(512)S(1)} %get-tuple-element.631, s32[1024]{0:T(1024)S(1)} %pad_clamp_fusion.5), kind=kCustom, calls=%fused_computation.12.clone | custom fusion | bytes 6144 | tf_op jit(solution)/shard_map/jit(_take)/gather | solution.py:60
  24.4 0.6 compare_select_fusion.4
  24.9 3.5 %gather_fusion.9 = s32[512]{0:T(512)S(1)} fusion(s32[512]{0:T(512)S(1)} %get-tuple-element.628, s32[1024]{0:T(1024)S(1)} %pad_clamp_fusion.4), kind=kCustom, calls=%fused_computation.13.clone | custom fusion | bytes 6144 | tf_op jit(solution)/shard_map/jit(_take)/gather | solution.py:60
  28.4 0.5 compare_select_fusion.3
  29.0 3.5 %gather_fusion.11 = s32[512]{0:T(512)S(1)} fusion(s32[512]{0:T(512)S(1)} %get-tuple-element.625, s32[1024]{0:T(1024)S(1)} %pad_clamp_fusion.3), kind=kCustom, calls=%fused_computation.14.clone | custom fusion | bytes 6144 | tf_op jit(solution)/shard_map/jit(_take)/gather | solution.py:60
  32.5 0.6 compare_select_fusion.2
  33.1 3.5 %gather_fusion.13 = s32[512]{0:T(512)S(1)} fusion(s32[512]{0:T(512)S(1)} %get-tuple-element.622, s32[1024]{0:T(1024)S(1)} %pad_clamp_fusion.2), kind=kCustom, calls=%fused_computation.15.clone | custom fusion | bytes 6144 | tf_op jit(solution)/shard_map/jit(_take)/gather | solution.py:60
  36.6 0.6 compare_select_fusion.1
  37.2 3.5 %gather_fusion.15 = s32[512]{0:T(512)S(1)} fusion(s32[512]{0:T(512)S(1)} %get-tuple-element.619, s32[1024]{0:T(1024)S(1)} %pad_clamp_fusion.1), kind=kCustom, calls=%fused_computation.16.clone | custom fusion | bytes 6144 | tf_op jit(solution)/shard_map/jit(_take)/gather | solution.py:60
  40.7 0.6 compare_and_fusion
  41.2 4.8 %all-gather.3 = bf16[2,168,45]{1,2,0:T(8,128)(2,1)S(1)} all-gather(bf16[1,168,45]{1,2,0:T(8,128)(2,1)S(1)} %get-tuple-element.675), channel_id=2, replica_groups=mesh['req_0'=8,'req_1'=4,'req_2'=2,'tp'=8] {'req_2'}, dimensions={0}, use_global_device_ids=true | all-gather | bytes 45360 | tf_op jit(solution)/shard_map/all_gather | solution.py:28
  46.0 9.4 %all-gather.4 = bf16[4,168,45]{1,2,0:T(8,128)(2,1)S(1)} all-gather(bf16[1,168,45]{1,2,0:T(8,128)(2,1)S(1)} %get-tuple-element.676), channel_id=3, replica_groups=mesh['req_0'=8,'req_1'=4,'req_2'=2,'tp'=8] {'req_1'}, dimensions={0}, use_global_device_ids=true | all-gather | bytes 75600 | tf_op jit(solution)/shard_map/all_gather | solution.py:28
  55.4 9.6 %all_gather.28 = bf16[8,168,45]{1,2,0:T(8,128)(2,1)S(1)} all-gather(bf16[2,168,45]{1,2,0:T(8,128)(2,1)S(1)} %all-gather.3), channel_id=1, replica_groups=mesh['req_0'=8,'req_1'=4,'req_2'=2,'tp'=8] {'req_1'}, dimensions={0}, use_global_device_ids=true | all-gather | bytes 151200 | tf_op jit(solution)/shard_map/all_gather | solution.py:28
  65.0 0.7 copy.102
  65.8 19.9 %all-gather.5 = bf16[8,176,45]{1,2,0:T(8,128)(2,1)S(1)} all-gather(bf16[1,176,45]{1,2,0:T(8,128)(2,1)S(1)} %slice_bitcast_fusion), channel_id=4, replica_groups=mesh['req_0'=8,'req_1'=4,'req_2'=2,'tp'=8] {'req_0'}, dimensions={0}, use_global_device_ids=true | all-gather | bytes 142560 | tf_op jit(solution)/shard_map/all_gather | solution.py:28
  85.8 5.1 %all_gather.34 = bf16[16,176,45]{1,0,2:T(8,128)(2,1)S(1)} all-gather(bf16[8,176,45]{1,0,2:T(8,128)(2,1)S(1)} %copy.105), channel_id=1, replica_groups=mesh['req_0'=8,'req_1'=4,'req_2'=2,'tp'=8] {'req_2'}, dimensions={0}, use_global_device_ids=true | all-gather | bytes 380160 | tf_op jit(solution)/shard_map/all_gather | solution.py:28
  90.8 1.0 copy.97
  91.8 19.8 %all_gather.31 = bf16[32,168,45]{1,2,0:T(8,128)(2,1)S(1)} all-gather(bf16[4,168,45]{1,2,0:T(8,128)(2,1)S(1)} %all-gather.4), channel_id=1, replica_groups=mesh['req_0'=8,'req_1'=4,'req_2'=2,'tp'=8] {'req_0'}, dimensions={0}, use_global_device_ids=true | all-gather | bytes 544320 | tf_op jit(solution)/shard_map/all_gather | solution.py:28
  111.9 11.4 %all_gather.32 = bf16[64,168,45]{1,0,2:T(8,128)(2,1)S(1)} all-gather(bf16[32,168,45]{1,0,2:T(8,128)(2,1)S(1)} %copy.103), channel_id=1, replica_groups=mesh['req_0'=8,'req_1'=4,'req_2'=2,'tp'=8] {'req_2'}, dimensions={0}, use_global_device_ids=true | all-gather | bytes 1451520 | tf_op jit(solution)/shard_map/all_gather | solution.py:28
  123.3 1.3 reshape.341
  124.6 4.0 %copy.119 = bf16[2,8,4,168,45]{3,0,2,1,4:T(2,128)(2,1)S(1)} copy(bf16[2,8,4,168,45]{3,2,1,0,4:T(4,128)(2,1)} %reshape.341) | data formatting | bytes 1935360 | tf_op jit(solution)/shard_map/reshape | solution.py:30
  128.6 2.3 reshape.342
  130.9 1.6 gather_fusion
  132.7 1.6 gather_fusion.2
  134.7 1.6 gather_fusion.4
  136.5 1.6 gather_fusion.6
  138.4 1.6 gather_fusion.8
  140.2 1.6 gather_fusion.10
  142.1 1.6 gather_fusion.12
  143.9 2.4 gather_fusion.14
  146.2 12.9 %all_gather.35 = bf16[64,176,45]{1,0,2:T(8,128)(2,1)S(1)} all-gather(bf16[16,176,45]{1,0,2:T(8,128)(2,1)S(1)} %all_gather.34), channel_id=1, replica_groups=mesh['req_0'=8,'req_1'=4,'req_2'=2,'tp'=8] {'req_1'}, dimensions={0}, use_global_device_ids=true | all-gather | bytes 1267200 | tf_op jit(solution)/shard_map/all_gather | solution.py:28
  159.1 2.6 copy.118
  161.7 4.6 %reshape.344 = bf16[64,176,45]{1,0,2:T(8,128)(2,1)} reshape(bf16[8,4,2,176,45]{3,2,1,0,4:T(2,128)(2,1)} %bitcast.614) | data formatting | bytes 2027520 | tf_op jit(solution)/shard_map/reshape | solution.py:32
  166.3 21.2 %all_gather.29 = bf16[64,168,45]{1,0,2:T(8,128)(2,1)S(1)} all-gather(bf16[8,168,45]{1,0,2:T(8,128)(2,1)S(1)} %copy-done.8), channel_id=1, replica_groups=mesh['req_0'=8,'req_1'=4,'req_2'=2,'tp'=8] {'req_0'}, dimensions={0}, use_global_device_ids=true | all-gather | bytes 1088640 | tf_op jit(solution)/shard_map/all_gather | solution.py:28
  187.5 2.4 maximum_bitcast_fusion
  189.9 3.3 %copy.107 = bf16[512,64,45]{0,2,1:T(8,128)(2,1)} copy(bf16[512,64,45]{0,1,2:T(8,128)(2,1)S(1)} %maximum_bitcast_fusion) | data formatting | bytes 5898240 | tf_op jit(solution)/shard_map/transpose | solution.py:36
  193.2 4.7 %reshape.345 = bf16[512,2880]{0,1:T(8,128)(2,1)} reshape(bf16[512,64,45]{0,2,1:T(8,128)(2,1)} %copy.107) | data formatting | bytes 5898240 | tf_op jit(solution)/shard_map/reshape | solution.py:38
  198.1 1.6 gather_fusion.16
  199.9 0.6 copy-done.4
  200.7 6.0 %conditional.6 = (bf16[128,512]{0,1:T(8,128)(2,1)S(1)}) conditional(s32[]{:T(128)} %bitcast.74, () %tuple.50, (bf16[1,1024,64]{1,2,0:T(8,128)(2,1)S(1)}, bf16[1,1024,64]{1,2,0:T(8,128)(2,1)S(1)}, bf16[512,512]{0,1:T(8,128)(2,1)}, s32[512,512]{1,0:T(8,128)S(1)}, bf16[512,1,64]{0,2,1:T(8,128)(2,1)S(1)}, ...), branch_computations={%region_16.19_spmd, %region_17.26_spmd} | conditional | flops 276973568 | bytes 17961200 | solution.py:166
  201.0 0.9 slice.26
  202.2 2.9 while.58
  203.1 0.5 fusion.225
  204.5 0.5 fusion.225
  206.7 5.8 %conditional.5 = (bf16[128,512]{0,1:T(8,128)(2,1)S(1)}) conditional(s32[]{:T(128)} %bitcast.73, () %tuple.49, (bf16[1,1024,64]{1,2,0:T(8,128)(2,1)S(1)}, bf16[1,1024,64]{1,2,0:T(8,128)(2,1)S(1)}, bf16[512,512]{0,1:T(8,128)(2,1)}, s32[512,512]{1,0:T(8,128)S(1)}, bf16[512,1,64]{0,2,1:T(8,128)(2,1)S(1)}, /*index=5*/bf16[512,1,64]{0,2,1:T(8,128)(2,1)S(1)}, ...), branch_computations={%region_8.11_spmd, %region_9.18_spmd} | conditional | flops 276973568 | bytes 17961200 | solution.py:166
  206.8 0.9 slice.24
  207.9 2.9 while.57
  208.8 0.5 fusion.231
  210.3 0.5 fusion.231
  212.5 5.8 %conditional.4 = (bf16[128,512]{0,1:T(8,128)(2,1)S(1)}) conditional(s32[]{:T(128)} %bitcast.68, () %tuple.47, (bf16[1,1024,64]{1,2,0:T(8,128)(2,1)S(1)}, bf16[1,1024,64]{1,2,0:T(8,128)(2,1)S(1)}, bf16[512,512]{0,1:T(8,128)(2,1)}, s32[512,512]{1,0:T(8,128)S(1)}, bf16[512,1,64]{0,2,1:T(8,128)(2,1)S(1)}, /*index=5*/bf16[512,1,64]{0,2,1:T(8,128)(2,1)S(1)}, ...), branch_computations={%region_0.3_spmd, %region_1.10_spmd} | conditional | flops 276973568 | bytes 17961200 | solution.py:166
  212.6 0.9 slice.22
  213.7 2.9 while.56
  214.6 0.5 fusion.237
  216.0 0.5 fusion.237
  217.8 0.5 fusion.27
  218.3 5.3 %convolution_convert_fusion = bf16[512,2880]{1,0:T(8,128)(2,1)} fusion(bf16[512,2880]{0,1:T(8,128)(2,1)} %reshape.345, bf16[128,512]{0,1:T(8,128)(2,1)S(1)} %get-tuple-element.1008, bf16[128,512]{0,1:T(8,128)(2,1)S(1)} %get-tuple-element.1007, bf16[128,512]{0,1:T(8,128)(2,1)S(1)} %get-tuple-element.1006, bf16[128,512]{0,1:T(8,128)(2,1)S(1)} %get-tuple-element.1005), kind=kOutput, calls=%fused_computation.257 | convolution fusion | flops 1513521152 | bytes 6422528 | tf_op jit(solution)/shard_map/dot_general | solution.py:173
  223.6 87.0 %reduce-scatter.2.cloned.1.call-done = bf16[64,2880]{1,0:T(8,128)(2,1)} async-done(((bf16[512,2880]{1,0:T(8,128)(2,1)}), bf16[64,2880]{1,0:T(8,128)(2,1)}) %reduce-scatter.2.cloned.1.call-update) | async-done | bytes 368656 | tf_op jit(solution)/shard_map/reduce_scatter | solution.py:176
  (130 shorter events, 12.7 us)
Async XLA Ops:
  6.5 3.2 %copy-start = (s32[1,512]{1,0:T(1,128)S(1)}, s32[1,512]{1,0:T(1,128)}, u32[]{:S(2)}) copy-start(s32[1,512]{1,0:T(1,128)} %param.35) | copy-start | bytes 6148
  6.5 304.1 %reduce-scatter.2.cloned.1.call-start = ((), (), s32[]{:S(2)}) async-start(), calls=%async_computation.1 | async-start | bytes 3391488 | tf_op jit(solution)/shard_map/reduce_scatter | solution.py:176
  36.6 54.3 %copy-start.9 = (bf16[1,512,512]{2,1,0:T(8,128)(2,1)S(1)}, bf16[1,512,512]{2,1,0:T(8,128)(2,1)}, u32[]{:S(2)}) copy-start(bf16[1,512,512]{2,1,0:T(8,128)(2,1)} %param.29) | copy-start | bytes 1572868
  134.7 1.6 copy-start.13
  136.5 1.6 copy-start.14
  138.4 1.6 copy-start.15
  140.2 1.6 copy-start.16
  142.0 1.6 copy-start.17
  161.7 4.6 %copy-start.8 = (bf16[8,168,45]{1,0,2:T(8,128)(2,1)S(1)}, bf16[8,168,45]{1,0,2:T(8,128)(2,1)}, u32[]{:S(2)}) copy-start(bf16[8,168,45]{1,0,2:T(8,128)(2,1)} %copy.102) | copy-start | bytes 362884
  161.7 25.7 %copy-start.1 = (bf16[64,168,45]{1,0,2:T(8,128)(2,1)S(1)}, bf16[64,168,45]{1,0,2:T(8,128)(2,1)}, u32[]{:S(2)}) copy-start(bf16[64,168,45]{1,0,2:T(8,128)(2,1)} %reshape.342) | copy-start | bytes 2903044
  166.3 21.2 %copy-start.2 = (bf16[64,176,45]{1,0,2:T(8,128)(2,1)S(1)}, bf16[64,176,45]{1,0,2:T(8,128)(2,1)}, u32[]{:S(2)}) copy-start(bf16[64,176,45]{1,0,2:T(8,128)(2,1)} %reshape.344) | copy-start | bytes 3041284
  193.2 4.7 %copy-start.3 = (s32[512,512]{1,0:T(8,128)S(1)}, s32[512,512]{1,0:T(8,128)}, u32[]{:S(2)}) copy-start(s32[512,512]{1,0:T(8,128)} %gather_fusion.14) | copy-start | bytes 3145732
  193.2 4.7 %copy-start.12 = (pred[512]{0:T(512)(128)(4,1)S(1)}, pred[512]{0:T(512)(128)(4,1)}, u32[]{:S(2)}) copy-start(pred[512]{0:T(512)(128)(4,1)} %get-tuple-element.617) | copy-start | bytes 1540
  198.0 1.7 copy-start.11
  199.7 0.9 copy-start.4
  199.7 1.0 copy-start.5
  199.7 1.0 copy-start.6
  199.7 1.0 copy-start.7
  199.7 1.0 copy-start.10
Sparse Core Ops, SparseCore 0:
  223.7 86.8 reduce-scatter.1
where the time goes:
time: 320 us; the launch traced here: 317 us
  blocking collectives  114 us (36%)
  waiting for transfers between devices  87 us (27%)
  local copies, waits for them, and re-layouts  74.9 us (23%)
  between operations  14.5 us (5%)
  matrix products  14.1 us (4%)
  other arithmetic  12 us (4%)
    all_gather x9, blocking collectives, all_blocks(): parts = lax.all_gather(parts, axes[k], axis=0, tiled=True)  114 us
    reduce_scatter x1, waiting for transfers between devices, per_device(): lax.psum_scatter(terms.astype(jnp.bfloat16), 'tp', scatter_dimension=0, t...  87 us
    gather x8, local copies, waits for them, and re-layouts, ancestry(): upward = jnp.take(upward, upward, axis=0)  27.9 us
    gather x9, local copies, waits for them, and re-layouts, ancestry(): visible = jnp.maximum(visible, jnp.take(visible, upward, axis=0))  15.3 us
    reshape x3, local copies, waits for them, and re-layouts, all_blocks(): parts = parts.reshape(*block, *x.shape)  7.96 us
    reshape x2, local copies, waits for them, and re-layouts, all_blocks(): parts.transpose(*turned, *range(len(order), parts.ndim))  6.86 us
  transfers between devices with their start and end apart: 1, of which 1 were waited for; matrix products, arithmetic and copies ran while one was open for 0% of the time, Pallas kernels for 0%

commit v1 on v0

v1 whole, which is shorter than its diff:
```python
import jax
import jax.numpy as jnp
from jax import lax
from jax.experimental import pallas as pl
from jax.experimental.pallas import tpu as pltpu
from jax.sharding import Mesh
from jax.sharding import PartitionSpec as P

HEADS = 64
KV_HEADS = 8
HEAD_DIM = 64
TREE = 512
TILE = 128
CTX = 1024
N_Y, N_X, N_ZL, N_ZH, N_CORE = 8, 4, 2, 4, 2
COLS = 45
PAD = 48
CUT = 16
K_DEV = 512
CHUNK_ROWS = ((0, 1), (-1, 2), (-2, 3), (-3, 4))
CHUNK = 2 * N_X * PAD
HALF = TILE // 2
masked_score = -1e30
MESH = pl.DeviceIdType.MESH
REQ = ("y", "x", "zl")
TP = ("zh", "core")
F32 = jnp.float32
BF16 = jnp.bfloat16


def nt(a, b):
    return lax.dot_general(a, b, (((1,), (1,)), ((), ())), preferred_element_type=F32)


def nn(a, b):
    return jnp.dot(a, b, preferred_element_type=F32)


def ids(shape, dim):
    return lax.broadcasted_iota(jnp.int32, shape, dim)


ROW_OFFSETS = (0, 1, -1, 2, -2, 3, -3, 4)
NAMES = (
    ["s0", "s1"]
    + ["ax" + k for k in "PMF"]
    + ["ay%d" % r for r in ROW_OFFSETS[1:]]
    + ["by%d" % r for r in ROW_OFFSETS[1:]]
    + ["bx%d%s" % (r, k) for r in ROW_OFFSETS for k in "PMF"]
    + ["at%d" % t for t in range(4)]
    + ["rs%d%d" % (c, k) for c in range(4) for k in range(6)]
    + ["fi%d" % c for c in range(4)]
)
INDEX = {name: i for i, name in enumerate(NAMES)}


def kernel(
    q_ref, tk_ref, tv_ref, ck_ref, cv_ref, sink_ref, par_ref, cnt_ref, w_ref,
    out_ref,
    wt, wg, k2, vx, bias, reach, att, snd, rcv, fin, hrecv, sel,
    send_sem, recv_sem, local_sem,
):
    y, x, zl = lax.axis_index("y"), lax.axis_index("x"), lax.axis_index("zl")
    zh, core = lax.axis_index("zh"), lax.axis_index("core")
    d = 1 - 2 * core

    def wrap(a, n):
        return lax.rem(a + n, n)

    xp, xm, xd = ({"x": wrap(x + s, N_X)} for s in (1, -1, d))
    yp, ym, yd = ({"y": wrap(y + s, N_Y)} for s in (1, -1, d))
    zp, zm = ({"zh": wrap(zh + s, N_ZH)} for s in (1, -1))
    partner = {"core": 1 - core}

    barrier = pltpu.get_barrier_semaphore()
    peers = [partner, xp, xm, yp, ym, zp, zm]
    peers += [{"zl": 1 - zl, "core": 0}, {"zl": 1 - zl, "core": 1}]
    for peer in peers:
        pl.semaphore_signal(barrier, inc=1, device_id=peer, device_id_type=MESH)

    pick = (ids((PAD, COLS), 0) == ids((PAD, COLS), 1)).astype(F32).astype(BF16)
    wt[...] = nt(pick, w_ref[...]).astype(BF16)
    pl.semaphore_wait(barrier, len(peers))

    started = []

    def copy(name, src, dst, device):
        i = INDEX[name]
        return pltpu.make_async_remote_copy(
            src_ref=src, dst_ref=dst, send_sem=send_sem.at[i], recv_sem=recv_sem.at[i],
            device_id=device, device_id_type=MESH,
        )

    def send(name, src, dst, device):
        one = copy(name, src, dst, device)
        one.start()
        started.append(one)

    def await_recv(name, dst):
        copy(name, dst, dst, partner).wait_recv()

    def slot(xx, yy):
        return 4 * wrap(yy, N_Y) + wrap(xx, N_X)

    own = slot(x, y)

    def lanes(k):
        return pl.ds(pl.multiple_of(k * K_DEV, K_DEV), K_DEV)

    mine = wg.at[own, :, lanes(core)]
    far = pltpu.make_async_remote_copy(
        src_ref=wt, dst_ref=mine, send_sem=send_sem.at[INDEX["s0"]],
        recv_sem=recv_sem.at[core], device_id={"zl": 1 - zl, "core": zl}, device_id_type=MESH,
    )
    far.start()
    near = pltpu.make_async_remote_copy(
        src_ref=wt, dst_ref=mine, send_sem=send_sem.at[INDEX["s1"]],
        recv_sem=recv_sem.at[core], device_id=partner, device_id_type=MESH,
    )
    here = pltpu.make_async_copy(wt, mine, local_sem)

    @pl.when(zl == core)
    def _():
        here.start()

    @pl.when(zl != core)
    def _():
        near.start()

    def a_block(xx, yy):
        return wg.at[slot(xx, yy), pl.ds(0, CUT), :]

    def a_row(yy):
        return wg.at[pl.ds(4 * wrap(yy, N_Y), 4), pl.ds(0, CUT), :]

    def b_block(xx, yy):
        return wg.at[slot(xx, yy), pl.ds(CUT, PAD - CUT), :]

    messages = {
        "axP": (a_block(x, y), a_block(x - 1, y), xp),
        "axM": (a_block(x, y), a_block(x + 1, y), xm),
        "axF": (a_block(x - d, y), a_block(x + 2, y), xd),
        "ay4": (a_row(y - 3 * d), a_row(y + 4), yd),
        "by4": (b_block(x, y - 3 * d), b_block(x, y + 4), yd),
    }
    for k in (1, 2, 3):
        messages["ay%d" % -k] = (a_row(y - k + 1), a_row(y - k), yp)
        messages["ay%d" % k] = (a_row(y + k - 1), a_row(y + k), ym)
        messages["by%d" % -k] = (b_block(x, y - k + 1), b_block(x, y - k), yp)
        messages["by%d" % k] = (b_block(x, y + k - 1), b_block(x, y + k), ym)
    for r in ROW_OFFSETS:
        messages["bx%dP" % r] = (b_block(x, y + r), b_block(x - 1, y + r), xp)
        messages["bx%dM" % r] = (b_block(x, y + r), b_block(x + 1, y + r), xm)
        messages["bx%dF" % r] = (b_block(x - d, y + r), b_block(x + 2, y + r), xd)

    def go(name):
        src, _, device = messages[name]
        send(name, src, src, device)

    def got(name):
        await_recv(name, messages[name][1])

    def begin_gather():
        for k in range(2):
            part = wg.at[own, :, pl.ds(k * K_DEV, K_DEV)]
            waiting = pltpu.make_async_remote_copy(
                src_ref=part, dst_ref=part, send_sem=send_sem.at[0], recv_sem=recv_sem.at[k],
                device_id=partner, device_id_type=MESH,
            )

            @pl.when((zl != core) | (core != k))
            def _():
                waiting.wait_recv()

        @pl.when(zl == core)
        def _():
            here.wait()

        for name in ("axP", "axM", "by1", "by-1", "bx0P", "bx0M"):
            go(name)

    def row_b(r):
        got("by%d" % r)
        if abs(r) < 3:
            go("by%d" % (r + (1 if r > 0 else -1)))
        go("bx%dP" % r)
        go("bx%dM" % r)

    def last_hop(kind):
        go("%sy4" % kind)

    def relay(r):
        got("bx%dP" % r)
        got("bx%dM" % r)
        go("bx%dF" % r)

    def row_a(r):
        got("ay%d" % r)
        if abs(r) < 3:
            go("ay%d" % (r + (1 if r > 0 else -1)))

    def g1():
        got("axP")
        got("axM")
        go("axF")

    def g2():
        row_b(1)
        row_b(-1)
        relay(0)

    def g3():
        got("axF")
        go("ay1")
        go("ay-1")

    def g4():
        row_b(2)
        row_b(-2)
        relay(1)
        relay(-1)

    def g5():
        row_a(1)
        row_a(-1)

    def g6():
        row_b(3)
        row_b(-3)
        last_hop("b")
        relay(2)
        relay(-2)

    def g7():
        row_a(2)
        row_a(-2)

    def g8():
        got("by4")
        go("bx4P")
        go("bx4M")
        relay(3)
        relay(-3)

    def g9():
        row_a(3)
        row_a(-3)
        last_hop("a")

    def g10():
        relay(4)

    def chunk_ready(c):
        for r in CHUNK_ROWS[c]:
            got("bx%dF" % r)
        if 4 in CHUNK_ROWS[c]:
            got("ay4")

    eye_k = (ids((HEAD_DIM, 2 * HEAD_DIM), 0) == ids((HEAD_DIM, 2 * HEAD_DIM), 1) % HEAD_DIM).astype(F32).astype(BF16)
    eye_v = (ids((HEAD_DIM, 2 * HEAD_DIM), 0) == ids((HEAD_DIM, 2 * HEAD_DIM), 1)).astype(F32).astype(BF16)
    ones_v = (ids((1, 2 * HEAD_DIM), 1) >= HEAD_DIM).astype(F32)
    for source, at, length in ((ck_ref, 0, CTX), (tk_ref, CTX, TREE)):
        k2[pl.ds(at, length), :] = nn(source[...], eye_k).astype(BF16)
    for source, at, length in ((cv_ref, 0, CTX), (tv_ref, CTX, TREE)):
        vx[pl.ds(at, length), :] = (nn(source[...], eye_v) + ones_v).astype(BF16)

    begin_gather()

    square = (TREE, TREE)
    eye = (ids(square, 0) == ids(square, 1)).astype(F32).astype(BF16)
    up = ((ids(square, 0) == par_ref[...]) | (ids(square, 0) == ids(square, 1))).astype(F32).astype(BF16)
    reach[...] = nt(eye, up).astype(BF16)

    def squaring(_, carry):
        twice = nn(reach[...], reach[...])
        reach[...] = (twice > 0.5).astype(F32).astype(BF16)
        return carry

    lax.fori_loop(0, 4, squaring, 0)
    g1()
    lax.fori_loop(0, 5, squaring, 0)
    bias[...] = jnp.where(reach[...].astype(F32) > 0.5, 0.0, masked_score)
    g2()
    g3()

    low = ids((TILE, TILE), 1) < HEAD_DIM
    live_tiles = cnt_ref[0]

    def tile_rows(t):
        return pl.ds(pl.multiple_of(t * TILE, TILE), TILE)

    def attend(t, n):
        rows = tile_rows(t)

        def pair(p, carry):
            columns = pl.ds(pl.multiple_of(p * TILE, TILE), TILE)
            both = q_ref[rows, columns].astype(F32) * (HEAD_DIM**-0.5)
            q2 = jnp.concatenate(
                [jnp.where(low, both, 0.0), jnp.where(low, 0.0, both)], axis=0
            ).astype(BF16)
            s_c = nt(q2, k2[pl.ds(0, CTX), :])
            mask = bias[rows, :]
            s_t = nt(q2, k2[pl.ds(CTX, TREE), :]) + jnp.concatenate([mask, mask], axis=0)
            first = ids((2 * TILE, 1), 0) < TILE
            sink = jnp.where(first, sink_ref[2 * p], sink_ref[2 * p + 1])
            peak = jnp.maximum(
                jnp.maximum(s_c.max(-1, keepdims=True), s_t.max(-1, keepdims=True)), sink
            )
            p_c = jnp.exp(s_c - peak).astype(BF16)
            p_t = jnp.exp(s_t - peak).astype(BF16)
            o = nn(p_c, vx[pl.ds(0, CTX), :]) + nn(p_t, vx[pl.ds(CTX, TREE), :])
            den = pltpu.roll(o, HEAD_DIM, 1) + jnp.exp(sink - peak)
            res = o / den
            odd = pltpu.roll(res[TILE:], HEAD_DIM, 1)
            res = jnp.where(low, res[:TILE], odd)
            res = jnp.where(t < live_tiles, res, 0.0)
            att[core, rows, columns] = res.astype(BF16)
            return carry

        lax.fori_loop(0, 4, pair, 0)
        part = att.at[core, rows, :]
        send("at%d" % n, part, part, partner)

    opp, up_t, dn_t = wrap(zh + 2, N_ZH), wrap(zh + 1, N_ZH), wrap(zh - 1, N_ZH)
    tiles = (opp, up_t, dn_t, zh)

    def att_ready(n):
        await_recv("at%d" % n, att.at[1 - core, tile_rows(tiles[n]), :])

    attend(opp, 0)
    g4()
    g5()
    attend(up_t, 1)
    g6()
    g7()
    attend(dn_t, 2)
    g8()
    g9()
    attend(zh, 3)
    g10()

    shape = (CHUNK, CHUNK)
    lane, column = ids(shape, 0), ids(shape, 1)
    for hf in range(2):
        inner = lane - hf * N_X * PAD
        block = sum((inner >= PAD * i).astype(jnp.int32) for i in (1, 2, 3))
        j = inner - PAD * block
        inside = (inner >= 0) & (inner < N_X * PAD) & (j < COLS)
        for z in range(N_ZL):
            hit = inside & (column == COLS * (2 * block + z) + j)
            sel[hf, z] = hit.astype(F32).astype(BF16)

    for n in range(4):
        att_ready(n)

    def project(t, c):
        a, b = CHUNK_ROWS[c]
        wa = wg[pl.ds(4 * wrap(y + a, N_Y), 4)].reshape(N_X * PAD, 2 * K_DEV)
        wb = wg[pl.ds(4 * wrap(y + b, N_Y), 4)].reshape(N_X * PAD, 2 * K_DEV)
        w = jnp.concatenate([wa, wb], axis=0)
        rows = tile_rows(t)
        return nt(att[0, rows, :], w[:, :K_DEV]) + nt(att[1, rows, :], w[:, K_DEV:])

    def ship(c, k, value, device):
        snd[c, k] = value.astype(BF16)
        send("rs%d%d" % (c, k), snd.at[c, k], rcv.at[c, k], device)

    def landed(c, k):
        await_recv("rs%d%d" % (c, k), rcv.at[c, k])
        return rcv[c, k].astype(F32)

    kept = {}

    def phase1(c):
        chunk_ready(c)
        value = project(opp, c)
        ship(c, 0, value[:HALF], zp)
        ship(c, 1, value[HALF:], zm)
        value = project(up_t, c)
        ship(c, 2, value[HALF:], zp)
        fin[0, c] = value[:HALF]
        value = project(dn_t, c)
        ship(c, 3, value[:HALF], zm)
        fin[1, c] = value[HALF:]

    def phase2(c):
        ship(c, 4, fin[0, c] + landed(c, 0), zp)
        ship(c, 5, fin[1, c] + landed(c, 1), zm)
        value = project(zh, c)
        fin[0, c] = value[:HALF]
        fin[1, c] = value[HALF:]

    def phase3(c):
        top = fin[0, c] + landed(c, 4) + landed(c, 3)
        low_half = fin[1, c] + landed(c, 5) + landed(c, 2)
        keep = jnp.where(core == 0, top, low_half).astype(BF16)
        give = jnp.where(core == 0, low_half, top).astype(BF16)
        hrecv[0, c] = keep
        hrecv[1, c] = give
        send("fi%d" % c, hrecv.at[1, c], hrecv.at[2, c], partner)

    def phase4(c):
        await_recv("fi%d" % c, hrecv.at[2, c])
        for hf in range(2):
            r = nn(hrecv[0, c], sel[hf, core]) + nn(hrecv[2, c], sel[hf, 1 - core])
            out_ref[wrap(y + CHUNK_ROWS[c][hf], N_Y)] = r[:, : N_X * 2 * COLS].astype(BF16)

    phase1(0)
    phase1(1)
    phase2(0)
    phase1(2)
    phase2(1)
    phase1(3)
    phase2(2)
    phase3(0)
    phase2(3)
    phase3(1)
    phase4(0)
    phase3(2)
    phase4(1)
    phase3(3)
    phase4(2)
    phase4(3)

    for one in started:
        one.wait_send()
    far.wait_send()

    @pl.when(zl != core)
    def _():
        near.wait_send()


def per_device(
    tree_queries, tree_keys, tree_values, cache_keys, cache_values, sinks, parents, tile_counts, out_weight
):
    vmem = pl.BlockSpec(memory_space=pltpu.VMEM)
    smem = pl.BlockSpec(memory_space=pltpu.SMEM)
    keys = CTX + TREE
    count = len(NAMES)
    out = pl.pallas_call(
        kernel,
        out_shape=jax.ShapeDtypeStruct((N_Y, HALF, N_X * 2 * COLS), BF16),
        in_specs=[vmem, vmem, vmem, vmem, vmem, smem, vmem, smem, vmem],
        out_specs=vmem,
        scratch_shapes=[
            pltpu.VMEM((PAD, K_DEV), BF16),
            pltpu.VMEM((N_Y * N_X, PAD, 2 * K_DEV), BF16),
            pltpu.VMEM((keys, 2 * HEAD_DIM), BF16),
            pltpu.VMEM((keys, 2 * HEAD_DIM), BF16),
            pltpu.VMEM((TREE, TREE), F32),
            pltpu.VMEM((TREE, TREE), BF16),
            pltpu.VMEM((2, TREE, K_DEV), BF16),
            pltpu.VMEM((4, 6, HALF, CHUNK), BF16),
            pltpu.VMEM((4, 6, HALF, CHUNK), BF16),
            pltpu.VMEM((2, 4, HALF, CHUNK), F32),
            pltpu.VMEM((3, 4, HALF, CHUNK), BF16),
            pltpu.VMEM((2, 2, CHUNK, CHUNK), BF16),
            pltpu.SemaphoreType.DMA((count,)),
            pltpu.SemaphoreType.DMA((count,)),
            pltpu.SemaphoreType.DMA,
        ],
        compiler_params=pltpu.CompilerParams(collective_id=0, has_side_effects=True),
    )(
        tree_queries[0], tree_keys[0], tree_values[0], cache_keys[0], cache_values[0],
        sinks, parents, tile_counts, out_weight,
    )
    return out.transpose(1, 0, 2).reshape(1, HALF, -1)


def solution(mesh):
    sizes = (N_Y, N_X, N_ZL, N_ZH, N_CORE)
    split = Mesh(mesh.devices.reshape(sizes), (*REQ, *TP))
    placed = (
        P(REQ, None, TP),
        P(REQ, None, TP),
        P(REQ, None, TP),
        P(REQ, None, TP),
        P(REQ, None, TP),
        P(TP),
        P(REQ, None),
        P(REQ),
        P(TP, REQ),
    )
    return jax.shard_map(
        per_device, mesh=split, in_specs=placed, out_specs=P(REQ, TP, None), check_vma=False
    )
```

time: 320 us -> 84.1 us (0.26)
  blocking collectives: 114 us -> 0 us
  waiting for transfers between devices: 87 us -> 0 us
  Pallas kernels: 0 us -> 75.8 us
  local copies, waits for them, and re-layouts: 74.9 us -> 7.3 us
  matrix products: 14.1 us -> 0 us
  between operations: 14.5 us -> 0.68 us
  other arithmetic: 12 us -> 0 us
    all_gather x9 -> x0, blocking collectives: 114 us -> none  [all_blocks(): parts = lax.all_gather(parts, axes[k], axis=0, tiled=True)]
    reduce_scatter x1 -> x0, waiting for transfers between devices: 87 us -> none  [per_device(): lax.psum_scatter(terms.astype(jnp.bfloat16), 'tp', scatter_dimension=0, t...]
    pallas_call x0 -> x1, Pallas kernels: none -> 75.8 us  [per_device(): pl.pallas_call(kernel, out_shape=jax.ShapeDtypeStruct((N_Y, HALF, N_X * 2...]
    gather x17 -> x0, local copies, waits for them, and re-layouts: 43.2 us -> none  [the longest x8 27.9 us: ancestry(): upward = jnp.take(upward, upward, axis=0)]
    reshape x6 -> x1, local copies, waits for them, and re-layouts: 19.5 us -> 1.05 us  [per_device(): return out.transpose(1, 0, 2).reshape(1, HALF, -1)]
    dot_general x19 -> x0, matrix products: 14.1 us -> none  [the longest x1 5.29 us: per_device(): jnp.dot(attention, spread_gather(out_weight, REQ, 1), preferred_element_t...]
    select_n x8 -> x0, other arithmetic: 3.53 us -> none  [ancestry(): visible = jnp.maximum(visible, jnp.take(visible, upward, axis=0))]
  transfers between devices with their start and end apart: 1 -> 0, of which waited for: 1 -> 0; matrix products, arithmetic and copies ran while one was open for 0% -> 0% of each run, Pallas kernels for 0% -> 0%
where the time goes in v1:
time: 84.1 us; the launch traced here: 83.8 us
  Pallas kernels  75.8 us (90%)
  local copies, waits for them, and re-layouts  7.3 us (9%)
    pallas_call x1, Pallas kernels, per_device(): pl.pallas_call(kernel, out_shape=jax.ShapeDtypeStruct((N_Y, HALF, N_X * 2...  75.8 us
    unnamed x13, local copies, waits for them, and re-layouts  5.02 us

profile of v1, /device:TPU:1, one launch (start us, length us, event | category | flops | bytes accessed | tf_op | source)
XLA Modules:
  0.0 83.8 jit_solution(16447947812000079883)
XLA Ops:
  0.7 0.0 copy-start.2
  0.7 1.6 %copy.15 = bf16[1,512,64]{2,1,0:T(8,128)(2,1)} copy(bf16[1,512,64]{1,2,0:T(8,128)(2,1)} %param.10) | data formatting | bytes 131072 | tf_op args[1]
  2.3 0.0 copy-done.2
  2.3 0.0 copy-start.3
  2.3 0.7 copy.16
  3.0 0.0 copy-start
  3.0 0.0 copy-done.3
  3.1 0.8 copy.19.w_ref
  3.9 0.1 copy-done
  3.9 0.0 copy-start.1
  3.9 0.8 %copy.17 = bf16[1,1024,64]{2,1,0:T(8,128)(2,1)} copy(bf16[1,1024,64]{1,2,0:T(8,128)(2,1)S(1)} %copy-done) | data formatting | bytes 262144 | tf_op args[3]
  4.8 0.1 copy-done.1
  4.9 0.8 copy.18
  5.7 75.8 %shard_map.91 = bf16[8,64,360]{2,1,0:T(8,128)(2,1)} custom-call(bf16[512,512]{1,0:T(8,128)(2,1)} %bitcast.9, bf16[512,64]{1,0:T(8,128)(2,1)} %bitcast.10, bf16[512,64]{1,0:T(8,128)(2,1)} %bitcast.11, bf16[1024,64]{1,0:T(8,128)(2,1)} %bitcast.7, bf16[1024,64]{1,0:T(8,128)(2,1)} %bitcast.8, f32[8]{0:T(128)} %sink_ref.1, s32[1,512]{1,0:T(1,128)} %par_ref.1, ...), custom_call_target="tpu_custom_call" | custom-call | tf_op jit(solution)/shard_map/pallas_call | solution.py:441
  81.5 1.2 %copy.20 = bf16[64,8,360]{2,1,0:T(8,128)(2,1)S(1)} copy(bf16[64,8,360]{2,0,1:T(8,128)(2,1)} %bitcast.6) | data formatting | bytes 737280 | tf_op jit(solution)/shard_map/transpose | solution.py:468
  82.8 1.0 %reshape.3 = bf16[1,64,2880]{2,1,0:T(8,128)(2,1)} reshape(bf16[64,8,360]{2,1,0:T(8,128)(2,1)S(1)} %copy.20) | data formatting | bytes 737280 | tf_op jit(solution)/shard_map/reshape | solution.py:468
Async XLA Ops:
  0.7 1.6 %copy-start.2 = (bf16[1,512,64]{1,2,0:T(8,128)(2,1)S(1)}, bf16[1,512,64]{1,2,0:T(8,128)(2,1)}, u32[]{:S(2)}) copy-start(bf16[1,512,64]{1,2,0:T(8,128)(2,1)} %param.11) | copy-start | bytes 196612
  2.3 0.8 copy-start.3
  3.0 0.9 %copy-start = (bf16[1,1024,64]{1,2,0:T(8,128)(2,1)S(1)}, bf16[1,1024,64]{1,2,0:T(8,128)(2,1)}, u32[]{:S(2)}) copy-start(bf16[1,1024,64]{1,2,0:T(8,128)(2,1)} %param.12) | copy-start | bytes 393220
  3.9 0.9 %copy-start.1 = (bf16[1,1024,64]{1,2,0:T(8,128)(2,1)S(1)}, bf16[1,1024,64]{1,2,0:T(8,128)(2,1)}, u32[]{:S(2)}) copy-start(bf16[1,1024,64]{1,2,0:T(8,128)(2,1)} %param.13) | copy-start | bytes 393220

commit v2 on v1

--- a/solution.py
+++ b/solution.py
@@ -20,6 +20,8 @@
 CHUNK_ROWS = ((0, 1), (-1, 2), (-2, 3), (-3, 4))
 CHUNK = 2 * N_X * PAD
 HALF = TILE // 2
+BLOCK = TREE // 2
+VROWS = HEAD_DIM + 16
 masked_score = -1e30
 MESH = pl.DeviceIdType.MESH
 REQ = ("y", "x", "zl")
@@ -57,7 +59,7 @@
 def kernel(
     q_ref, tk_ref, tv_ref, ck_ref, cv_ref, sink_ref, par_ref, cnt_ref, w_ref,
     out_ref,
-    wt, wg, k2, vx, bias, reach, att, snd, rcv, fin, hrecv, sel,
+    wt, wg, k2, vx, bias, reach, att, snd, rcv, fin, hrecv, sel, res_rows,
     send_sem, recv_sem, local_sem,
 ):
     y, x, zl = lax.axis_index("y"), lax.axis_index("x"), lax.axis_index("zl")
@@ -78,8 +80,8 @@
     for peer in peers:
         pl.semaphore_signal(barrier, inc=1, device_id=peer, device_id_type=MESH)
 
-    pick = (ids((PAD, COLS), 0) == ids((PAD, COLS), 1)).astype(F32).astype(BF16)
-    wt[...] = nt(pick, w_ref[...]).astype(BF16)
+    block = w_ref[...].astype(F32)
+    wt[...] = jnp.concatenate([block, jnp.zeros((PAD - COLS, K_DEV), F32)], axis=0).astype(BF16)
     pl.semaphore_wait(barrier, len(peers))
 
     started = []
@@ -204,21 +206,10 @@
         got("axM")
         go("axF")
 
-    def g2():
-        row_b(1)
-        row_b(-1)
-        relay(0)
-
     def g3():
         got("axF")
         go("ay1")
         go("ay-1")
-
-    def g4():
-        row_b(2)
-        row_b(-2)
-        relay(1)
-        relay(-1)
 
     def g5():
         row_a(1)
@@ -256,32 +247,43 @@
         if 4 in CHUNK_ROWS[c]:
             got("ay4")
 
-    eye_k = (ids((HEAD_DIM, 2 * HEAD_DIM), 0) == ids((HEAD_DIM, 2 * HEAD_DIM), 1) % HEAD_DIM).astype(F32).astype(BF16)
-    eye_v = (ids((HEAD_DIM, 2 * HEAD_DIM), 0) == ids((HEAD_DIM, 2 * HEAD_DIM), 1)).astype(F32).astype(BF16)
-    ones_v = (ids((1, 2 * HEAD_DIM), 1) >= HEAD_DIM).astype(F32)
     for source, at, length in ((ck_ref, 0, CTX), (tk_ref, CTX, TREE)):
-        k2[pl.ds(at, length), :] = nn(source[...], eye_k).astype(BF16)
-    for source, at, length in ((cv_ref, 0, CTX), (tv_ref, CTX, TREE)):
-        vx[pl.ds(at, length), :] = (nn(source[...], eye_v) + ones_v).astype(BF16)
+        keys = source[...].astype(F32)
+        k2[pl.ds(at, length), :] = jnp.concatenate([keys, keys], axis=0).T.astype(BF16)
+    vx[pl.ds(0, HEAD_DIM), pl.ds(0, CTX)] = cv_ref[...]
+    vx[pl.ds(0, HEAD_DIM), pl.ds(CTX, TREE)] = tv_ref[...]
+    vx[pl.ds(HEAD_DIM, VROWS - HEAD_DIM), :] = jnp.ones((VROWS - HEAD_DIM, CTX + TREE), BF16)
+
+    square = (BLOCK, BLOCK)
+
+    def parent_of(j0, i0):
+        return (ids(square, 0) + j0) == par_ref[:, pl.ds(i0, BLOCK)]
+
+    for i in range(2):
+        edge = parent_of(i * BLOCK, i * BLOCK) | (ids(square, 0) == ids(square, 1))
+        reach[i] = edge.astype(F32).astype(BF16)
 
     begin_gather()
 
-    square = (TREE, TREE)
-    eye = (ids(square, 0) == ids(square, 1)).astype(F32).astype(BF16)
-    up = ((ids(square, 0) == par_ref[...]) | (ids(square, 0) == ids(square, 1))).astype(F32).astype(BF16)
-    reach[...] = nt(eye, up).astype(BF16)
-
     def squaring(_, carry):
-        twice = nn(reach[...], reach[...])
-        reach[...] = (twice > 0.5).astype(F32).astype(BF16)
+        twice = [nn(reach[i], reach[i]) for i in range(2)]
+        for i in range(2):
+            reach[i] = (twice[i] > 0.5).astype(F32).astype(BF16)
         return carry
 
     lax.fori_loop(0, 4, squaring, 0)
     g1()
-    lax.fori_loop(0, 5, squaring, 0)
-    bias[...] = jnp.where(reach[...].astype(F32) > 0.5, 0.0, masked_score)
-    g2()
-    g3()
+    lax.fori_loop(0, 4, squaring, 0)
+    across = nn(reach[0], parent_of(0, BLOCK).astype(F32).astype(BF16)).astype(BF16)
+    across = nn(across, reach[1])
+
+    def as_bias(seen):
+        return jnp.where(seen.astype(F32) > 0.5, 0.0, masked_score)
+
+    bias[pl.ds(0, BLOCK), pl.ds(0, BLOCK)] = as_bias(reach[0])
+    bias[pl.ds(0, BLOCK), pl.ds(BLOCK, BLOCK)] = as_bias(across)
+    bias[pl.ds(BLOCK, BLOCK), pl.ds(0, BLOCK)] = jnp.full(square, masked_score, F32)
+    bias[pl.ds(BLOCK, BLOCK), pl.ds(BLOCK, BLOCK)] = as_bias(reach[1])
 
     low = ids((TILE, TILE), 1) < HEAD_DIM
     live_tiles = cnt_ref[0]
@@ -289,37 +291,34 @@
     def tile_rows(t):
         return pl.ds(pl.multiple_of(t * TILE, TILE), TILE)
 
-    def attend(t, n):
+    def attend(t, n, half):
         rows = tile_rows(t)
-
-        def pair(p, carry):
-            columns = pl.ds(pl.multiple_of(p * TILE, TILE), TILE)
+        mask = bias[:, rows]
+        mask = jnp.concatenate([mask, mask], axis=1)
+        for p in (2 * half, 2 * half + 1):
+            columns = pl.ds(p * TILE, TILE)
             both = q_ref[rows, columns].astype(F32) * (HEAD_DIM**-0.5)
             q2 = jnp.concatenate(
                 [jnp.where(low, both, 0.0), jnp.where(low, 0.0, both)], axis=0
             ).astype(BF16)
-            s_c = nt(q2, k2[pl.ds(0, CTX), :])
-            mask = bias[rows, :]
-            s_t = nt(q2, k2[pl.ds(CTX, TREE), :]) + jnp.concatenate([mask, mask], axis=0)
-            first = ids((2 * TILE, 1), 0) < TILE
+            s_c = nt(k2[pl.ds(0, CTX), :], q2)
+            s_t = nt(k2[pl.ds(CTX, TREE), :], q2) + mask
+            first = ids((1, 2 * TILE), 1) < TILE
             sink = jnp.where(first, sink_ref[2 * p], sink_ref[2 * p + 1])
             peak = jnp.maximum(
-                jnp.maximum(s_c.max(-1, keepdims=True), s_t.max(-1, keepdims=True)), sink
+                jnp.maximum(s_c.max(0, keepdims=True), s_t.max(0, keepdims=True)), sink
             )
             p_c = jnp.exp(s_c - peak).astype(BF16)
             p_t = jnp.exp(s_t - peak).astype(BF16)
-            o = nn(p_c, vx[pl.ds(0, CTX), :]) + nn(p_t, vx[pl.ds(CTX, TREE), :])
-            den = pltpu.roll(o, HEAD_DIM, 1) + jnp.exp(sink - peak)
-            res = o / den
-            odd = pltpu.roll(res[TILE:], HEAD_DIM, 1)
-            res = jnp.where(low, res[:TILE], odd)
+            o = nn(vx[:, pl.ds(0, CTX)], p_c) + nn(vx[:, pl.ds(CTX, TREE)], p_t)
+            den = o[HEAD_DIM : HEAD_DIM + 1] + jnp.exp(sink - peak)
+            res = o[:HEAD_DIM] / den
+            res = jnp.concatenate([res[:, :TILE], res[:, TILE:]], axis=0).T
             res = jnp.where(t < live_tiles, res, 0.0)
             att[core, rows, columns] = res.astype(BF16)
-            return carry
-
-        lax.fori_loop(0, 4, pair, 0)
-        part = att.at[core, rows, :]
-        send("at%d" % n, part, part, partner)
+        if half:
+            part = att.at[core, rows, :]
+            send("at%d" % n, part, part, partner)
 
     opp, up_t, dn_t = wrap(zh + 2, N_ZH), wrap(zh + 1, N_ZH), wrap(zh - 1, N_ZH)
     tiles = (opp, up_t, dn_t, zh)
@@ -327,17 +326,24 @@
     def att_ready(n):
         await_recv("at%d" % n, att.at[1 - core, tile_rows(tiles[n]), :])
 
-    attend(opp, 0)
-    g4()
+    attend(opp, 0, 0)
+    row_b(1)
+    row_b(-1)
+    attend(opp, 0, 1)
+    relay(0)
+    attend(up_t, 1, 0)
+    g3()
+    attend(up_t, 1, 1)
+    row_b(2)
+    row_b(-2)
+    attend(dn_t, 2, 0)
+    relay(1)
+    relay(-1)
+    attend(dn_t, 2, 1)
     g5()
-    attend(up_t, 1)
+    attend(zh, 3, 0)
     g6()
-    g7()
-    attend(dn_t, 2)
-    g8()
-    g9()
-    attend(zh, 3)
-    g10()
+    attend(zh, 3, 1)
 
     shape = (CHUNK, CHUNK)
     lane, column = ids(shape, 0), ids(shape, 1)
@@ -403,13 +409,17 @@
         await_recv("fi%d" % c, hrecv.at[2, c])
         for hf in range(2):
             r = nn(hrecv[0, c], sel[hf, core]) + nn(hrecv[2, c], sel[hf, 1 - core])
-            out_ref[wrap(y + CHUNK_ROWS[c][hf], N_Y)] = r[:, : N_X * 2 * COLS].astype(BF16)
+            res_rows[wrap(y + CHUNK_ROWS[c][hf], N_Y)] = r.astype(BF16)
 
     phase1(0)
+    g7()
     phase1(1)
     phase2(0)
+    g8()
+    g9()
     phase1(2)
     phase2(1)
+    g10()
     phase1(3)
     phase2(2)
     phase3(0)
@@ -421,6 +431,9 @@
     phase3(3)
     phase4(2)
     phase4(3)
+    width = N_X * 2 * COLS
+    for i in range(N_Y):
+        out_ref[:, pl.ds(width * i, width)] = res_rows[i][:, :width]
 
     for one in started:
         one.wait_send()
@@ -440,32 +453,33 @@
     count = len(NAMES)
     out = pl.pallas_call(
         kernel,
-        out_shape=jax.ShapeDtypeStruct((N_Y, HALF, N_X * 2 * COLS), BF16),
+        out_shape=jax.ShapeDtypeStruct((HALF, N_Y * N_X * 2 * COLS), BF16),
         in_specs=[vmem, vmem, vmem, vmem, vmem, smem, vmem, smem, vmem],
         out_specs=vmem,
         scratch_shapes=[
             pltpu.VMEM((PAD, K_DEV), BF16),
             pltpu.VMEM((N_Y * N_X, PAD, 2 * K_DEV), BF16),
             pltpu.VMEM((keys, 2 * HEAD_DIM), BF16),
-            pltpu.VMEM((keys, 2 * HEAD_DIM), BF16),
+            pltpu.VMEM((VROWS, keys), BF16),
             pltpu.VMEM((TREE, TREE), F32),
-            pltpu.VMEM((TREE, TREE), BF16),
+            pltpu.VMEM((2, BLOCK, BLOCK), BF16),
             pltpu.VMEM((2, TREE, K_DEV), BF16),
             pltpu.VMEM((4, 6, HALF, CHUNK), BF16),
             pltpu.VMEM((4, 6, HALF, CHUNK), BF16),
             pltpu.VMEM((2, 4, HALF, CHUNK), F32),
             pltpu.VMEM((3, 4, HALF, CHUNK), BF16),
             pltpu.VMEM((2, 2, CHUNK, CHUNK), BF16),
+            pltpu.VMEM((N_Y, HALF, CHUNK), BF16),
             pltpu.SemaphoreType.DMA((count,)),
             pltpu.SemaphoreType.DMA((count,)),
             pltpu.SemaphoreType.DMA,
         ],
         compiler_params=pltpu.CompilerParams(collective_id=0, has_side_effects=True),
     )(
-        tree_queries[0], tree_keys[0], tree_values[0], cache_keys[0], cache_values[0],
-        sinks, parents, tile_counts, out_weight,
+        tree_queries[0], tree_keys[0].T, tree_values[0].T, cache_keys[0].T, cache_values[0].T,
+        sinks, parents, tile_counts, out_weight.T,
     )
-    return out.transpose(1, 0, 2).reshape(1, HALF, -1)
+    return out[None]
 
 
 def solution(mesh):

time: 84.1 us -> 74.9 us (0.89)
  local copies, waits for them, and re-layouts: 7.3 us -> 1.76 us
  Pallas kernels: 75.8 us -> 72.3 us
    pallas_call x1, Pallas kernels: 75.8 us -> 72.3 us  [per_device(): pl.pallas_call(kernel, out_shape=jax.ShapeDtypeStruct((HALF, N_Y * N_X *...]
    unnamed x13 -> x1, local copies, waits for them, and re-layouts: 5.02 us -> 1.76 us
    transpose x1 -> x0, local copies, waits for them, and re-layouts: 1.23 us -> none  [per_device(): return out.transpose(1, 0, 2).reshape(1, HALF, -1)]
    reshape x1 -> x0, local copies, waits for them, and re-layouts: 1.05 us -> none  [per_device(): return out.transpose(1, 0, 2).reshape(1, HALF, -1)]
where the time goes in v2:
time: 74.9 us; the launch traced here: 74.8 us
  Pallas kernels  72.3 us (97%)
  local copies, waits for them, and re-layouts  1.76 us (2%)
    pallas_call x1, Pallas kernels, per_device(): pl.pallas_call(kernel, out_shape=jax.ShapeDtypeStruct((HALF, N_Y * N_X *...  72.3 us
    unnamed x1, local copies, waits for them, and re-layouts  1.76 us

profile of v2, /device:TPU:1, one launch (start us, length us, event | category | flops | bytes accessed | tf_op | source)
XLA Modules:
  0.0 74.8 jit_solution(8826483730211703603)
XLA Ops:
  0.7 72.3 %shard_map.91 = bf16[64,2880]{1,0:T(8,128)(2,1)} custom-call(bf16[512,512]{1,0:T(8,128)(2,1)} %bitcast.16, bf16[64,512]{1,0:T(8,128)(2,1)} %bitcast.19, bf16[64,512]{1,0:T(8,128)(2,1)} %bitcast.20, bf16[64,1024]{1,0:T(8,128)(2,1)} %bitcast.17, bf16[64,1024]{1,0:T(8,128)(2,1)} %bitcast.18, f32[8]{0:T(128)} %sink_ref.1, s32[1,512]{1,0:T(1,128)} %par_ref.1, ...), custom_call_target="tpu_custom_call" | custom-call | tf_op jit(solution)/shard_map/pallas_call | solution.py:454
  73.0 1.8 %copy.12 = bf16[1,64,2880]{2,1,0:T(8,128)(2,1)} copy(bf16[1,64,2880]{2,1,0:T(8,128)(2,1)} %bitcast.15) | data formatting | bytes 737280

commit v3 on v2

--- a/solution.py
+++ b/solution.py
@@ -17,7 +17,6 @@
 PAD = 48
 CUT = 16
 K_DEV = 512
-CHUNK_ROWS = ((0, 1), (-1, 2), (-2, 3), (-3, 4))
 CHUNK = 2 * N_X * PAD
 HALF = TILE // 2
 BLOCK = TREE // 2
@@ -46,9 +45,9 @@
 NAMES = (
     ["s0", "s1"]
     + ["ax" + k for k in "PMF"]
-    + ["ay%d" % r for r in ROW_OFFSETS[1:]]
-    + ["by%d" % r for r in ROW_OFFSETS[1:]]
-    + ["bx%d%s" % (r, k) for r in ROW_OFFSETS for k in "PMF"]
+    + ["ay%d" % r for r in range(-3, 5) if r]
+    + ["by%d" % r for r in range(-3, 5) if r]
+    + ["bx%d%s" % (r, k) for r in range(-3, 5) for k in "PMF"]
     + ["at%d" % t for t in range(4)]
     + ["rs%d%d" % (c, k) for c in range(4) for k in range(6)]
     + ["fi%d" % c for c in range(4)]
@@ -59,7 +58,7 @@
 def kernel(
     q_ref, tk_ref, tv_ref, ck_ref, cv_ref, sink_ref, par_ref, cnt_ref, w_ref,
     out_ref,
-    wt, wg, k2, vx, bias, reach, att, snd, rcv, fin, hrecv, sel, res_rows,
+    wt, wg, k2, vx, bias, reach, att, snd, rcv, fin, hrecv, sel, res_rows, score_a, score_b,
     send_sem, recv_sem, local_sem,
 ):
     y, x, zl = lax.axis_index("y"), lax.axis_index("x"), lax.axis_index("zl")
@@ -84,22 +83,14 @@
     wt[...] = jnp.concatenate([block, jnp.zeros((PAD - COLS, K_DEV), F32)], axis=0).astype(BF16)
     pl.semaphore_wait(barrier, len(peers))
 
-    started = []
-
-    def copy(name, src, dst, device):
-        i = INDEX[name]
+    def copy(i, src, dst, device):
         return pltpu.make_async_remote_copy(
             src_ref=src, dst_ref=dst, send_sem=send_sem.at[i], recv_sem=recv_sem.at[i],
             device_id=device, device_id_type=MESH,
         )
 
-    def send(name, src, dst, device):
-        one = copy(name, src, dst, device)
-        one.start()
-        started.append(one)
-
-    def await_recv(name, dst):
-        copy(name, dst, dst, partner).wait_recv()
+    def await_recv(i, dst):
+        copy(i, dst, dst, partner).wait_recv()
 
     def slot(xx, yy):
         return 4 * wrap(yy, N_Y) + wrap(xx, N_X)
@@ -157,10 +148,10 @@
 
     def go(name):
         src, _, device = messages[name]
-        send(name, src, src, device)
+        copy(INDEX[name], src, src, device).start()
 
     def got(name):
-        await_recv(name, messages[name][1])
+        await_recv(INDEX[name], messages[name][1])
 
     def begin_gather():
         for k in range(2):
@@ -241,12 +232,6 @@
     def g10():
         relay(4)
 
-    def chunk_ready(c):
-        for r in CHUNK_ROWS[c]:
-            got("bx%dF" % r)
-        if 4 in CHUNK_ROWS[c]:
-            got("ay4")
-
     for source, at, length in ((ck_ref, 0, CTX), (tk_ref, CTX, TREE)):
         keys = source[...].astype(F32)
         k2[pl.ds(at, length), :] = jnp.concatenate([keys, keys], axis=0).T.astype(BF16)
@@ -286,157 +271,228 @@
     bias[pl.ds(BLOCK, BLOCK), pl.ds(BLOCK, BLOCK)] = as_bias(reach[1])
 
     low = ids((TILE, TILE), 1) < HEAD_DIM
+    first = ids((1, 2 * TILE), 1) < TILE
     live_tiles = cnt_ref[0]
+    opp, up_t, dn_t = wrap(zh + 2, N_ZH), wrap(zh + 1, N_ZH), wrap(zh - 1, N_ZH)
+
+    def tile_at(n):
+        shift = jnp.where(n == 0, 2, jnp.where(n == 1, 1, jnp.where(n == 2, 3, 0)))
+        return lax.rem(zh + shift, N_ZH)
 
     def tile_rows(t):
         return pl.ds(pl.multiple_of(t * TILE, TILE), TILE)
 
-    def attend(t, n, half):
+    def columns_of(u):
+        return pl.ds(pl.multiple_of(lax.rem(u, 4) * TILE, TILE), TILE)
+
+    def sink_of(u):
+        p = lax.rem(u, 4)
+        return jnp.where(first, sink_ref[2 * p], sink_ref[2 * p + 1])
+
+    def scores(u, store):
+        rows = tile_rows(tile_at(u // 4))
+        both = q_ref[rows, columns_of(u)].astype(F32) * (HEAD_DIM**-0.5)
+        q2 = jnp.concatenate(
+            [jnp.where(low, both, 0.0), jnp.where(low, 0.0, both)], axis=0
+        ).astype(BF16)
+        top = None
+        for i in range((CTX + TREE) // BLOCK):
+            s = nt(k2[pl.ds(i * BLOCK, BLOCK), :], q2)
+            if i * BLOCK >= CTX:
+                mask = bias[pl.ds(i * BLOCK - CTX, BLOCK), rows]
+                s = s + jnp.concatenate([mask, mask], axis=1)
+            store[pl.ds(i * BLOCK, BLOCK), :] = s
+            part = s.reshape(BLOCK // 8, 8, 2 * TILE).max(0)
+            top = part if top is None else jnp.maximum(top, part)
+        return jnp.maximum(top.max(0, keepdims=True), sink_of(u))
+
+    def weigh(u, store, peak):
+        t = tile_at(u // 4)
+        o = None
+        for i in range((CTX + TREE) // BLOCK):
+            keys = pl.ds(i * BLOCK, BLOCK)
+            p = jnp.exp(store[keys, :] - peak).astype(BF16)
+            part = nn(vx[:, keys], p)
+            o = part if o is None else o + part
+        den = o[HEAD_DIM : HEAD_DIM + 1] + jnp.exp(sink_of(u) - peak)
+        res = o[:HEAD_DIM] / den
+        res = jnp.concatenate([res[:, :TILE], res[:, TILE:]], axis=0).T
+        res = jnp.where(t < live_tiles, res, 0.0)
+        att[core, tile_rows(t), columns_of(u)] = res.astype(BF16)
+
+    def att_copy(n):
+        part = att.at[core, tile_rows(tile_at(n)), :]
+        return copy(INDEX["at0"] + n, part, part, partner)
+
+    def att_ready(n):
+        await_recv(INDEX["at0"] + n, att.at[1 - core, tile_rows(tile_at(n)), :])
+
+    def step_1():
+        row_b(1)
+        row_b(-1)
+
+    def step_2():
+        relay(0)
+
+    def step_4():
+        row_b(2)
+        row_b(-2)
+        relay(1)
+        relay(-1)
+
+    events = {0: step_1, 1: step_2, 2: g3, 4: step_4, 6: g5, 7: g6}
+
+    def attend(k, peak):
+        u = 2 * k
+        peak_b = scores(u + 1, score_b)
+        weigh(u, score_a, peak)
+        peak_a = scores(jnp.minimum(u + 2, 15), score_a)
+        weigh(u + 1, score_b, peak_b)
+
+        @pl.when(lax.rem(k, 2) == 1)
+        def _():
+            att_copy(k // 2).start()
+
+        for when, event in events.items():
+            pl.when(k == when)(event)
+        return peak_a
+
+    lax.fori_loop(0, 8, attend, scores(0, score_a))
+
+    def row_pair(c):
+        return -c, c + 1
+
+    def project(t, c):
+        parts = [
+            wg[pl.ds(4 * wrap(y + r, N_Y), 4)].reshape(N_X * PAD, 2 * K_DEV)
+            for r in row_pair(c)
+        ]
+        w = jnp.concatenate(parts, axis=0)
         rows = tile_rows(t)
-        mask = bias[:, rows]
-        mask = jnp.concatenate([mask, mask], axis=1)
-        for p in (2 * half, 2 * half + 1):
-            columns = pl.ds(p * TILE, TILE)
-            both = q_ref[rows, columns].astype(F32) * (HEAD_DIM**-0.5)
-            q2 = jnp.concatenate(
-                [jnp.where(low, both, 0.0), jnp.where(low, 0.0, both)], axis=0
-            ).astype(BF16)
-            s_c = nt(k2[pl.ds(0, CTX), :], q2)
-            s_t = nt(k2[pl.ds(CTX, TREE), :], q2) + mask
-            first = ids((1, 2 * TILE), 1) < TILE
-            sink = jnp.where(first, sink_ref[2 * p], sink_ref[2 * p + 1])
-            peak = jnp.maximum(
-                jnp.maximum(s_c.max(0, keepdims=True), s_t.max(0, keepdims=True)), sink
-            )
-            p_c = jnp.exp(s_c - peak).astype(BF16)
-            p_t = jnp.exp(s_t - peak).astype(BF16)
-            o = nn(vx[:, pl.ds(0, CTX)], p_c) + nn(vx[:, pl.ds(CTX, TREE)], p_t)
-            den = o[HEAD_DIM : HEAD_DIM + 1] + jnp.exp(sink - peak)
-            res = o[:HEAD_DIM] / den
-            res = jnp.concatenate([res[:, :TILE], res[:, TILE:]], axis=0).T
-            res = jnp.where(t < live_tiles, res, 0.0)
-            att[core, rows, columns] = res.astype(BF16)
-        if half:
-            part = att.at[core, rows, :]
-            send("at%d" % n, part, part, partner)
-
-    opp, up_t, dn_t = wrap(zh + 2, N_ZH), wrap(zh + 1, N_ZH), wrap(zh - 1, N_ZH)
-    tiles = (opp, up_t, dn_t, zh)
-
-    def att_ready(n):
-        await_recv("at%d" % n, att.at[1 - core, tile_rows(tiles[n]), :])
-
-    attend(opp, 0, 0)
-    row_b(1)
-    row_b(-1)
-    attend(opp, 0, 1)
-    relay(0)
-    attend(up_t, 1, 0)
-    g3()
-    attend(up_t, 1, 1)
-    row_b(2)
-    row_b(-2)
-    attend(dn_t, 2, 0)
-    relay(1)
-    relay(-1)
-    attend(dn_t, 2, 1)
-    g5()
-    attend(zh, 3, 0)
-    g6()
-    attend(zh, 3, 1)
-
-    shape = (CHUNK, CHUNK)
-    lane, column = ids(shape, 0), ids(shape, 1)
-    for hf in range(2):
-        inner = lane - hf * N_X * PAD
-        block = sum((inner >= PAD * i).astype(jnp.int32) for i in (1, 2, 3))
-        j = inner - PAD * block
-        inside = (inner >= 0) & (inner < N_X * PAD) & (j < COLS)
-        for z in range(N_ZL):
-            hit = inside & (column == COLS * (2 * block + z) + j)
-            sel[hf, z] = hit.astype(F32).astype(BF16)
+        return nt(att[0, rows, :], w[:, :K_DEV]) + nt(att[1, rows, :], w[:, K_DEV:])
+
+    routes = (zp, zm, zp, zm, zp, zm)
+
+    def rs_copy(c, k):
+        return copy(INDEX["rs00"] + 6 * c + k, snd.at[c, k], rcv.at[c, k], routes[k])
+
+    def ship(c, k, value):
+        snd[c, k] = value.astype(BF16)
+        rs_copy(c, k).start()
+
+    def landed(c, k):
+        await_recv(INDEX["rs00"] + 6 * c + k, rcv.at[c, k])
+        return rcv[c, k].astype(F32)
+
+    def fi_copy(c):
+        return copy(INDEX["fi0"] + c, hrecv.at[1, c], hrecv.at[2, c], partner)
+
+    def phase1(c):
+        for r in row_pair(c):
+            yy = y + r
+            await_recv(INDEX["bx0F"] + 3 * r, b_block(x + 2, yy))
+
+        def one(n, carry):
+            value = project(tile_at(n), c)
+
+            @pl.when(n == 0)
+            def _():
+                ship(c, 0, value[:HALF])
+                ship(c, 1, value[HALF:])
+
+            @pl.when(n == 1)
+            def _():
+                ship(c, 2, value[HALF:])
+                fin[0, c] = value[:HALF]
+
+            @pl.when(n == 2)
+            def _():
+                ship(c, 3, value[:HALF])
+                fin[1, c] = value[HALF:]
+
+            @pl.when(n == 3)
+            def _():
+                fin[2, c] = value[:HALF]
+                fin[3, c] = value[HALF:]
+
+            return carry
+
+        lax.fori_loop(0, 4, one, 0)
+
+    def phase2(c):
+        ship(c, 4, fin[0, c] + landed(c, 0))
+        ship(c, 5, fin[1, c] + landed(c, 1))
+
+    def phase3(c):
+        top = fin[2, c] + landed(c, 4) + landed(c, 3)
+        low_half = fin[3, c] + landed(c, 5) + landed(c, 2)
+        hrecv[0, c] = jnp.where(core == 0, top, low_half).astype(BF16)
+        hrecv[1, c] = jnp.where(core == 0, low_half, top).astype(BF16)
+        fi_copy(c).start()
+
+    def phase4(c):
+        await_recv(INDEX["fi0"] + c, hrecv.at[2, c])
+        for hf in range(2):
+            r = nn(hrecv[0, c], sel[hf, core]) + nn(hrecv[2, c], sel[hf, 1 - core])
+            res_rows[wrap(y + row_pair(c)[hf], N_Y)] = r.astype(BF16)
+
+    def make_selection():
+        shape = (CHUNK, CHUNK)
+
+        def one(n, carry):
+            hf, z = n // 2, lax.rem(n, 2)
+            inner = ids(shape, 0) - hf * N_X * PAD
+            block = sum((inner >= PAD * i).astype(jnp.int32) for i in (1, 2, 3))
+            j = inner - PAD * block
+            inside = (inner >= 0) & (inner < N_X * PAD) & (j < COLS)
+            target = jnp.where(inside, COLS * (2 * block + z) + j, -1)
+            sel[hf, z] = (ids(shape, 1) == target).astype(F32).astype(BF16)
+            return carry
+
+        lax.fori_loop(0, 4, one, 0)
 
     for n in range(4):
         att_ready(n)
 
-    def project(t, c):
-        a, b = CHUNK_ROWS[c]
-        wa = wg[pl.ds(4 * wrap(y + a, N_Y), 4)].reshape(N_X * PAD, 2 * K_DEV)
-        wb = wg[pl.ds(4 * wrap(y + b, N_Y), 4)].reshape(N_X * PAD, 2 * K_DEV)
-        w = jnp.concatenate([wa, wb], axis=0)
-        rows = tile_rows(t)
-        return nt(att[0, rows, :], w[:, :K_DEV]) + nt(att[1, rows, :], w[:, K_DEV:])
-
-    def ship(c, k, value, device):
-        snd[c, k] = value.astype(BF16)
-        send("rs%d%d" % (c, k), snd.at[c, k], rcv.at[c, k], device)
-
-    def landed(c, k):
-        await_recv("rs%d%d" % (c, k), rcv.at[c, k])
-        return rcv[c, k].astype(F32)
-
-    kept = {}
-
-    def phase1(c):
-        chunk_ready(c)
-        value = project(opp, c)
-        ship(c, 0, value[:HALF], zp)
-        ship(c, 1, value[HALF:], zm)
-        value = project(up_t, c)
-        ship(c, 2, value[HALF:], zp)
-        fin[0, c] = value[:HALF]
-        value = project(dn_t, c)
-        ship(c, 3, value[:HALF], zm)
-        fin[1, c] = value[HALF:]
-
-    def phase2(c):
-        ship(c, 4, fin[0, c] + landed(c, 0), zp)
-        ship(c, 5, fin[1, c] + landed(c, 1), zm)
-        value = project(zh, c)
-        fin[0, c] = value[:HALF]
-        fin[1, c] = value[HALF:]
-
-    def phase3(c):
-        top = fin[0, c] + landed(c, 4) + landed(c, 3)
-        low_half = fin[1, c] + landed(c, 5) + landed(c, 2)
-        keep = jnp.where(core == 0, top, low_half).astype(BF16)
-        give = jnp.where(core == 0, low_half, top).astype(BF16)
-        hrecv[0, c] = keep
-        hrecv[1, c] = give
-        send("fi%d" % c, hrecv.at[1, c], hrecv.at[2, c], partner)
-
-    def phase4(c):
-        await_recv("fi%d" % c, hrecv.at[2, c])
-        for hf in range(2):
-            r = nn(hrecv[0, c], sel[hf, core]) + nn(hrecv[2, c], sel[hf, 1 - core])
-            res_rows[wrap(y + CHUNK_ROWS[c][hf], N_Y)] = r.astype(BF16)
-
-    phase1(0)
-    g7()
-    phase1(1)
-    phase2(0)
-    g8()
-    g9()
-    phase1(2)
-    phase2(1)
-    g10()
-    phase1(3)
-    phase2(2)
-    phase3(0)
-    phase2(3)
-    phase3(1)
-    phase4(0)
-    phase3(2)
-    phase4(1)
-    phase3(3)
-    phase4(2)
-    phase4(3)
+    def step(i, carry):
+        @pl.when(i == 1)
+        def _():
+            g7()
+
+        @pl.when(i == 2)
+        def _():
+            g8()
+            g9()
+
+        @pl.when(i == 3)
+        def _():
+            g10()
+            got("ay4")
+
+        pl.when(i < 4)(lambda: phase1(i))
+        pl.when(i == 0)(make_selection)
+        pl.when((i >= 1) & (i < 5))(lambda: phase2(i - 1))
+        pl.when((i >= 3) & (i < 7))(lambda: phase3(i - 3))
+        pl.when(i >= 4)(lambda: phase4(i - 4))
+        return carry
+
+    lax.fori_loop(0, 8, step, 0)
+
     width = N_X * 2 * COLS
     for i in range(N_Y):
         out_ref[:, pl.ds(width * i, width)] = res_rows[i][:, :width]
 
-    for one in started:
-        one.wait_send()
+    for name, (src, _, device) in messages.items():
+        copy(INDEX[name], src, src, device).wait_send()
+
+    def drain(c, carry):
+        att_copy(c).wait_send()
+        fi_copy(c).wait_send()
+        for k in range(6):
+            rs_copy(c, k).wait_send()
+        return carry
+
+    lax.fori_loop(0, 4, drain, 0)
     far.wait_send()
 
     @pl.when(zl != core)
@@ -466,10 +522,12 @@
             pltpu.VMEM((2, TREE, K_DEV), BF16),
             pltpu.VMEM((4, 6, HALF, CHUNK), BF16),
             pltpu.VMEM((4, 6, HALF, CHUNK), BF16),
-            pltpu.VMEM((2, 4, HALF, CHUNK), F32),
+            pltpu.VMEM((4, 4, HALF, CHUNK), F32),
             pltpu.VMEM((3, 4, HALF, CHUNK), BF16),
             pltpu.VMEM((2, 2, CHUNK, CHUNK), BF16),
             pltpu.VMEM((N_Y, HALF, CHUNK), BF16),
+            pltpu.VMEM((keys, 2 * TILE), F32),
+            pltpu.VMEM((keys, 2 * TILE), F32),
             pltpu.SemaphoreType.DMA((count,)),
             pltpu.SemaphoreType.DMA((count,)),
             pltpu.SemaphoreType.DMA,

time: 74.9 us -> 67.8 us (0.905)
  Pallas kernels: 72.3 us -> 65.2 us
    pallas_call x1, Pallas kernels: 72.3 us -> 65.2 us  [per_device(): pl.pallas_call(kernel, out_shape=jax.ShapeDtypeStruct((HALF, N_Y * N_X *...]
where the time goes in v3:
time: 67.8 us; the launch traced here: 67.6 us
  Pallas kernels  65.2 us (96%)
  local copies, waits for them, and re-layouts  1.76 us (3%)
    pallas_call x1, Pallas kernels, per_device(): pl.pallas_call(kernel, out_shape=jax.ShapeDtypeStruct((HALF, N_Y * N_X *...  65.2 us
    unnamed x1, local copies, waits for them, and re-layouts  1.76 us

profile of v3, /device:TPU:1, one launch (start us, length us, event | category | flops | bytes accessed | tf_op | source)
XLA Modules:
  0.0 67.6 jit_solution(1937894856617480009)
XLA Ops:
  0.7 65.2 %shard_map.91 = bf16[64,2880]{1,0:T(8,128)(2,1)} custom-call(bf16[512,512]{1,0:T(8,128)(2,1)} %bitcast.16, bf16[64,512]{1,0:T(8,128)(2,1)} %bitcast.19, bf16[64,512]{1,0:T(8,128)(2,1)} %bitcast.20, bf16[64,1024]{1,0:T(8,128)(2,1)} %bitcast.17, bf16[64,1024]{1,0:T(8,128)(2,1)} %bitcast.18, f32[8]{0:T(128)} %sink_ref.1, s32[1,512]{1,0:T(1,128)} %par_ref.1, ...), custom_call_target="tpu_custom_call" | custom-call | tf_op jit(solution)/shard_map/pallas_call | solution.py:510
  65.8 1.8 %copy.12 = bf16[1,64,2880]{2,1,0:T(8,128)(2,1)} copy(bf16[1,64,2880]{2,1,0:T(8,128)(2,1)} %bitcast.15) | data formatting | bytes 737280

commit v4 on v3

--- a/solution.py
+++ b/solution.py
@@ -469,14 +469,21 @@
             g10()
             got("ay4")
 
-        pl.when(i < 4)(lambda: phase1(i))
+        phase1(i)
         pl.when(i == 0)(make_selection)
-        pl.when((i >= 1) & (i < 5))(lambda: phase2(i - 1))
-        pl.when((i >= 3) & (i < 7))(lambda: phase3(i - 3))
-        pl.when(i >= 4)(lambda: phase4(i - 4))
+        pl.when(i >= 1)(lambda: phase2(i - 1))
         return carry
 
-    lax.fori_loop(0, 8, step, 0)
+    lax.fori_loop(0, 4, step, 0)
+    phase3(0)
+    phase3(1)
+    phase4(0)
+    phase2(3)
+    phase4(1)
+    phase3(2)
+    phase4(2)
+    phase3(3)
+    phase4(3)
 
     width = N_X * 2 * COLS
     for i in range(N_Y):

time: 67.8 us -> 67.7 us (level)
  the two profiles are of different devices: /device:TPU:1 before, /device:TPU:25 now
where the time goes in v4:
time: 67.7 us; the launch traced here: 67.5 us
  Pallas kernels  65.1 us (96%)
  local copies, waits for them, and re-layouts  1.76 us (3%)
    pallas_call x1, Pallas kernels, per_device(): pl.pallas_call(kernel, out_shape=jax.ShapeDtypeStruct((HALF, N_Y * N_X *...  65.1 us
    unnamed x1, local copies, waits for them, and re-layouts  1.76 us

profile of v4, /device:TPU:25, one launch (start us, length us, event | category | flops | bytes accessed | tf_op | source)
XLA Modules:
  0.0 67.5 jit_solution(10854487772816792508)
XLA Ops:
  0.7 65.1 %shard_map.91 = bf16[64,2880]{1,0:T(8,128)(2,1)} custom-call(bf16[512,512]{1,0:T(8,128)(2,1)} %bitcast.16, bf16[64,512]{1,0:T(8,128)(2,1)} %bitcast.19, bf16[64,512]{1,0:T(8,128)(2,1)} %bitcast.20, bf16[64,1024]{1,0:T(8,128)(2,1)} %bitcast.17, bf16[64,1024]{1,0:T(8,128)(2,1)} %bitcast.18, f32[8]{0:T(128)} %sink_ref.1, s32[1,512]{1,0:T(1,128)} %par_ref.1, ...), custom_call_target="tpu_custom_call" | custom-call | tf_op jit(solution)/shard_map/pallas_call | solution.py:517
  65.7 1.8 %copy.12 = bf16[1,64,2880]{2,1,0:T(8,128)(2,1)} copy(bf16[1,64,2880]{2,1,0:T(8,128)(2,1)} %bitcast.15) | data formatting | bytes 737280
